TPU v7x, 32 devices: a whole 2x2x4 slice. The times are simulated.
32 devices in a mesh: chan: 16 (over z, y, core), wall: 2 (over x).
Axes of the slice: x: 2, y: 2, z: 4, core: 2. Of those that a mesh axis runs over, the one named last changes fastest.
Arguments:
- coords: float32 [3, 16, 2, 4096], P(None, 'chan', 'wall'), as said below
- masses: float32 [16, 2, 4096], P('chan', 'wall'), may hold values from 0.5 to 2
- counts: int32 [16, 2, 16], P('chan', 'wall'), may hold values from 64 to 256
- lists: int32 [16, 2, 5, 16, 2], P('chan', 'wall'), may hold values from 0 to 47, as said below
Outputs:
- density: float32 [16, 2, 4096], P('chan', 'wall')
Inputs may be any that keep to these rules, and one draw needn't show every extreme that they name: `lists`: each row of 2 entries names different tiles; tile t of extended slab s is s * 16 + t, slab 0 the lower cross-wall neighbour, 1 the slab itself, 2 the upper neighbour. `coords`: channel components lie in [0, 1), cross-wall and depth components in [0, 8).
All inputs are finite; a program needn't handle non-finite values.
Results may differ from a plain program's by a relative error of at most 0.0003.
Values sent between devices are 32-bit elements; how exact they have to be, the bound alone decides.
A program may use at most 64 MiB of HBM per device.

v0:
```python
import functools
import math

import jax
import jax.numpy as jnp
from jax import lax
from jax.experimental import pallas as pl
from jax.experimental.pallas import tpu as pltpu
from jax.sharding import PartitionSpec as P

NB = 2
R = 4
LANES = 128
ROWS = 64
MESH = pl.DeviceIdType.MESH


def wall_cases(wall, walls, flip):
    cases = []
    for s in range(3):
        other = wall + (1 - s if flip else s - 1)
        cases.append((s, other, jnp.logical_and(other >= 0, other < walls)))
    return cases


def gather_kernel(chans, walls, own_ref, ext_ref, send_sem, recv_sem, local_sem):
    chan = lax.axis_index("chan")
    wall = lax.axis_index("wall")
    valid = 1 + (wall > 0).astype(jnp.int32) + (wall < walls - 1).astype(jnp.int32)
    keep = pltpu.make_async_copy(own_ref, ext_ref.at[1], local_sem)
    keep.start()
    barrier = pltpu.get_barrier_semaphore()
    for s, other, there in wall_cases(wall, walls, False):
        @pl.when(there)
        def _(s=s, other=other):
            for k in range(R + 1):
                if k == 0 and s == 1:
                    continue
                pl.semaphore_signal(
                    barrier, inc=1, device_id=(lax.rem(chan + k, chans), other), device_id_type=MESH
                )
    pl.semaphore_wait(barrier, (R + 1) * valid - 1)

    def copy(k, s, other):
        return pltpu.make_async_remote_copy(
            src_ref=own_ref,
            dst_ref=ext_ref.at[k * 3 + s],
            send_sem=send_sem.at[k * 3 + s],
            recv_sem=recv_sem.at[k * 3 + s],
            device_id=(lax.rem(chan + chans - k, chans), other),
            device_id_type=MESH,
        )

    for k in range(R, -1, -1):
        for s, other, there in wall_cases(wall, walls, True):
            if k == 0 and s == 1:
                continue

            @pl.when(there)
            def _(k=k, s=s, other=other):
                copy(k, s, other).start()

    for k in range(R + 1):
        for s, other, there in wall_cases(wall, walls, False):
            if k == 0 and s == 1:
                continue

            @pl.when(there)
            def _(k=k, s=s, other=other):
                copy(k, s, other).wait_recv()

    for k in range(R + 1):
        for s, other, there in wall_cases(wall, walls, True):
            if k == 0 and s == 1:
                continue

            @pl.when(there)
            def _(k=k, s=s, other=other):
                copy(k, s, other).wait_send()
    keep.wait()


def gather(own, chans, walls):
    slots = (R + 1) * 3
    return pl.pallas_call(
        functools.partial(gather_kernel, chans, walls),
        out_shape=jax.ShapeDtypeStruct((slots,) + own.shape, own.dtype),
        in_specs=[pl.BlockSpec(memory_space=pltpu.VMEM)],
        out_specs=pl.BlockSpec(memory_space=pl.ANY),
        scratch_shapes=[
            pltpu.SemaphoreType.DMA((slots,)),
            pltpu.SemaphoreType.DMA((slots,)),
            pltpu.SemaphoreType.DMA,
        ],
        compiler_params=pltpu.CompilerParams(collective_id=0, has_side_effects=True),
    )(own)


def pair_kernel(
    walls,
    lists_ref,
    counts_ref,
    own_ref,
    ext_ref,
    gained_ref,
    handed_ref,
    cols,
    gacc,
    gains,
    hands,
    used,
    blocks_ref,
    sem,
):
    tiles, _, tile_len = own_ref.shape
    lane_blocks = tile_len // LANES
    list_len = lists_ref.shape[0] // ((R + 1) * tiles)
    wall = lax.axis_index("wall")
    filled = jnp.zeros((ext_ref.shape[0], LANES), jnp.float32)
    for h in range(lane_blocks):
        filled += (ext_ref[:, 3, h * LANES : (h + 1) * LANES] > 0.0).astype(jnp.float32)
    used[...] = jnp.transpose(filled, (1, 0))[:8].astype(jnp.int32)
    fetch = pltpu.make_async_copy(used, blocks_ref, sem)
    fetch.start()
    hands[...] = jnp.zeros_like(hands)
    fetch.wait()

    def own_tile(t, carry):
        turned = jnp.transpose(own_ref[t], (1, 0))
        for i in range(4):
            scale = 1.0 / R if i < 3 else 1.0
            cols[i] = jnp.broadcast_to(turned[:, i : i + 1] * scale, (tile_len, LANES))
        gacc[...] = jnp.zeros_like(gacc)
        groups = (counts_ref[t] + (ROWS - 1)) // ROWS

        def partner(m, carry):
            k = m // list_len
            j = m - k * list_len
            tile = lists_ref[(k * tiles + t) * list_len + j]
            at = k * 3 * tiles + tile
            slab = tile // tiles
            edge = wall + slab - 1
            real = jnp.logical_and(edge >= 0, edge < walls)
            blocks = jnp.where(real, blocks_ref[0, at], 0)
            lift = (slab - 1).astype(jnp.float32) * 2.0
            ahead = k.astype(jnp.float32) * (1.0 / R)

            def run(width):
                row = ext_ref[at]
                lanes = [pl.ds(h * LANES, LANES) for h in range(width)]

                def spread(i, h, scale, shift):
                    value = row[i : i + 1, h * LANES : (h + 1) * LANES]
                    if scale is not None:
                        value = value * scale + shift
                    return jnp.broadcast_to(value, (8, LANES))

                theirs = [
                    (
                        spread(0, h, 1.0 / R, ahead),
                        spread(1, h, 1.0 / R, lift),
                        spread(2, h, 1.0 / R, 0.0),
                        spread(3, h, None, None),
                    )
                    for h in range(width)
                ]

                def rows(g, sums):
                    sums = list(sums)
                    base = g * ROWS
                    for r in range(0, ROWS, 8):
                        here = pl.ds(pl.multiple_of(base + r, 8), 8)
                        ax, ay, az, aw = (cols[i, here, :] for i in range(4))
                        total = None
                        for h in range(width):
                            bx, by, bz, bw = theirs[h]
                            dx, dy, dz = ax - bx, ay - by, az - bz
                            square = dx * dx + dy * dy + (dz * dz + 0.0001 / (R * R))
                            q = square * lax.rsqrt(square)
                            outer = jnp.maximum(2.0 - q, 0.0)
                            inner = jnp.maximum(1.0 - q, 0.0)
                            weight = outer * outer * outer - (inner * inner) * (inner * 4.0)
                            part = weight * bw
                            total = part if total is None else total + part
                            sums[h] = sums[h] + weight * aw
                        gacc[here, :] += total
                    return tuple(sums)

                zero = jnp.zeros((8, LANES), jnp.float32)
                sums = lax.fori_loop(0, groups, rows, (zero,) * width)
                for h in range(width):
                    hands[at, :, lanes[h]] += sums[h]

            for width in range(1, lane_blocks + 1):
                pl.when(blocks == width)(functools.partial(run, width))
            return carry

        lax.fori_loop(0, (R + 1) * list_len, partner, 0)
        gains[t] = jnp.sum(
            jnp.transpose(gacc[...], (1, 0)).reshape(LANES // 8, 8, tile_len), axis=0
        )
        return carry

    lax.fori_loop(0, tiles, own_tile, 0)
    gained_ref[...] = jnp.sum(gains[...], axis=1)
    handed_ref[...] = jnp.sum(hands[...], axis=1)


def pairs(lists, counts, own, ext, walls):
    tiles, _, tile_len = own.shape
    smem = pl.BlockSpec(memory_space=pltpu.SMEM)
    vmem = pl.BlockSpec(memory_space=pltpu.VMEM)
    return pl.pallas_call(
        functools.partial(pair_kernel, walls),
        out_shape=(
            jax.ShapeDtypeStruct((tiles, tile_len), jnp.float32),
            jax.ShapeDtypeStruct((ext.shape[0], tile_len), jnp.float32),
        ),
        in_specs=[smem, smem, vmem, vmem],
        out_specs=(vmem, vmem),
        scratch_shapes=[
            pltpu.VMEM((4, tile_len, LANES), jnp.float32),
            pltpu.VMEM((tile_len, LANES), jnp.float32),
            pltpu.VMEM((tiles, 8, tile_len), jnp.float32),
            pltpu.VMEM((ext.shape[0], 8, tile_len), jnp.float32),
            pltpu.VMEM((8, ext.shape[0]), jnp.int32),
            pltpu.SMEM((8, ext.shape[0]), jnp.int32),
            pltpu.SemaphoreType.DMA,
        ],
    )(lists, counts, own, ext)


def return_kernel(chans, walls, tiles, gained_ref, handed_ref, out_ref, held, send_sem, recv_sem):
    chan = lax.axis_index("chan")
    wall = lax.axis_index("wall")
    valid = 1 + (wall > 0).astype(jnp.int32) + (wall < walls - 1).astype(jnp.int32)
    barrier = pltpu.get_barrier_semaphore()
    for s, other, there in wall_cases(wall, walls, True):
        @pl.when(there)
        def _(s=s, other=other):
            for k in range(1, R + 1):
                pl.semaphore_signal(
                    barrier,
                    inc=1,
                    device_id=(lax.rem(chan + chans - k, chans), other),
                    device_id_type=MESH,
                )
    pl.semaphore_wait(barrier, R * valid)

    def copy(k, s, other):
        slot = (k - 1) * 3 + s
        return pltpu.make_async_remote_copy(
            src_ref=handed_ref.at[pl.ds((k * 3 + s) * tiles, tiles)],
            dst_ref=held.at[slot],
            send_sem=send_sem.at[slot],
            recv_sem=recv_sem.at[slot],
            device_id=(lax.rem(chan + k, chans), other),
            device_id_type=MESH,
        )

    for k in range(R, 0, -1):
        for s, other, there in wall_cases(wall, walls, False):
            @pl.when(there)
            def _(k=k, s=s, other=other):
                copy(k, s, other).start()

    out_ref[...] = gained_ref[...]
    for k in range(1, R + 1):
        for s, other, there in wall_cases(wall, walls, True):
            @pl.when(there)
            def _(k=k, s=s, other=other):
                copy(k, s, other).wait_recv()
                out_ref[...] += held[(k - 1) * 3 + s]

    for k in range(1, R + 1):
        for s, other, there in wall_cases(wall, walls, False):
            @pl.when(there)
            def _(k=k, s=s, other=other):
                copy(k, s, other).wait_send()


def hand_back(gained, handed, chans, walls):
    tiles, tile_len = gained.shape
    vmem = pl.BlockSpec(memory_space=pltpu.VMEM)
    return pl.pallas_call(
        functools.partial(return_kernel, chans, walls, tiles),
        out_shape=jax.ShapeDtypeStruct(gained.shape, gained.dtype),
        in_specs=[vmem, vmem],
        out_specs=vmem,
        scratch_shapes=[
            pltpu.VMEM((R * 3, tiles, tile_len), jnp.float32),
            pltpu.SemaphoreType.DMA((R * 3,)),
            pltpu.SemaphoreType.DMA((R * 3,)),
        ],
        compiler_params=pltpu.CompilerParams(collective_id=1, has_side_effects=True),
    )(gained, handed)


def on_device(chans, walls, coords, masses, counts, lists):
    tiles = counts.shape[2]
    tile_len = masses.shape[2] // tiles
    slots = jnp.arange(tile_len, dtype=jnp.int32)
    filled = (slots[None, :] < counts[0, 0][:, None]).astype(jnp.float32)
    weighted = masses.reshape(tiles, tile_len) * filled
    own = jnp.concatenate([coords.reshape(3, tiles, tile_len), weighted[None]], axis=0)
    own = jnp.moveaxis(own, 0, 1)
    ext = gather(own, chans, walls)
    gained, handed = pairs(
        lists.reshape(-1), counts.reshape(-1), own, ext.reshape(-1, 4, tile_len), walls
    )
    total = hand_back(gained, handed, chans, walls)
    scale = 1.0 / (4.0 * math.pi * NB * tile_len)
    return (total * filled * scale).reshape(1, 1, -1)


def solution(mesh):
    placed = (
        P(None, "chan", "wall", None),
        P("chan", "wall", None),
        P("chan", "wall", None),
        P("chan", "wall", None, None, None),
    )
    body = functools.partial(on_device, mesh.shape["chan"], mesh.shape["wall"])
    return jax.shard_map(
        body, mesh=mesh, in_specs=placed, out_specs=P("chan", "wall", None), check_vma=False
    )
```

profile of v0, /device:TPU:0, one launch (start us, length us, event | category | flops | bytes accessed | tf_op | source)
XLA Modules:
  0.0 70.5 jit_solution(8059788153973683535)
XLA Ops:
  0.0 0.0 copy-start.2
  0.0 0.7 copy-done.2
  0.7 0.0 copy-start.1
  0.7 0.8 %compare_select_fusion = f32[1,16,256]{2,0,1:T(1,128)S(1)} fusion(f32[1,16,256]{2,0,1:T(1,128)} %bitcast.10, s32[16]{0:T(128)S(1)} %bitcast.12), kind=kLoop, calls=%fused_computation.1 | loop fusion | flops 8192 | bytes 32832 | tf_op jit(solution)/shard_map/mul | solution.py:304
  1.5 0.0 copy-done.1
  1.5 0.0 copy-start
  1.5 0.1 copy.5
  1.6 0.7 %reshape.65.lists_ref = s32[160]{0:T(256)} reshape(s32[1,1,5,16,2]{4,3,2,1,0:T(8,128)S(1)} %copy.5) | data formatting | bytes 1280 | tf_op jit(solution)/shard_map/reshape | solution.py:309
  2.3 0.0 copy-done
  2.3 0.1 reduce
  2.5 0.7 maximum_bitcast_fusion.own_ref
  3.1 18.4 %shard_map.46 = f32[15,16,4,256]{3,2,1,0:T(4,128)} custom-call(f32[16,4,256]{2,1,0:T(4,128)} %maximum_bitcast_fusion.own_ref), custom_call_target="tpu_custom_call" | custom-call | tf_op jit(solution)/shard_map/pallas_call | solution.py:85
  21.6 35.1 %shard_map.47 = (f32[16,256]{1,0:T(8,128)}, f32[240,256]{1,0:T(8,128)}) custom-call(s32[160]{0:T(256)} %reshape.65.lists_ref, s32[16]{0:T(128)} %bitcast.11, f32[16,4,256]{2,1,0:T(4,128)} %maximum_bitcast_fusion.own_ref, f32[240,4,256]{2,1,0:T(4,128)} %bitcast.8), custom_call_target="tpu_custom_call" | custom-call | tf_op jit(solution)/shard_map/pallas_call | solution.py:213
  56.7 0.0 copy-start.3
  56.7 12.4 %shard_map.48 = f32[16,256]{1,0:T(8,128)} custom-call(f32[16,256]{1,0:T(8,128)} %get-tuple-element.7.gained_ref, f32[240,256]{1,0:T(8,128)} %get-tuple-element.8.handed_ref), custom_call_target="tpu_custom_call" | custom-call | tf_op jit(solution)/shard_map/pallas_call | solution.py:285
  69.1 0.0 copy-done.3
  69.1 0.8 %select_multiply_fusion = f32[16,256]{1,0:T(8,128)S(1)} fusion(f32[16,256]{1,0:T(8,128)} %shard_map.48, s32[16]{0:T(128)S(1)} %bitcast.13), kind=kLoop, calls=%fused_computation.2 | loop fusion | flops 12288 | bytes 32832 | tf_op jit(solution)/shard_map/mul | solution.py:313
  69.9 0.6 reshape.69
Async XLA Ops:
  0.0 0.7 copy-start.2
  0.7 0.8 %copy-start.1 = (s32[1,1,5,16,2]{3,4,2,1,0:T(2,128)S(1)}, s32[1,1,5,16,2]{3,4,2,1,0:T(2,128)}, u32[]{:S(2)}) copy-start(s32[1,1,5,16,2]{3,4,2,1,0:T(2,128)} %param.7) | copy-start | bytes 1924
  1.5 0.8 %copy-start = (f32[3,1,1,4096]{3,2,1,0:T(1,128)S(1)}, f32[3,1,1,4096]{3,2,1,0:T(1,128)}, u32[]{:S(2)}) copy-start(f32[3,1,1,4096]{3,2,1,0:T(1,128)} %param.4) | copy-start | bytes 147460
  56.7 12.4 %copy-start.3 = (s32[1,1,16]{2,1,0:T(1,128)S(1)}, s32[1,1,16]{2,1,0:T(1,128)}, u32[]{:S(2)}) copy-start(s32[1,1,16]{2,1,0:T(1,128)} %param.6) | copy-start | bytes 196
where the time goes:
time: 71.3 us; the launch traced here: 70.5 us
  Pallas kernels  66 us (93%)
  other arithmetic  2.39 us (3%)
  local copies, waits for them, and re-layouts  2.12 us (3%)
    pallas_call x1, Pallas kernels, pairs(): pl.pallas_call(functools.partial(pair_kernel, walls), out_shape=(jax.Shap...  35.1 us
    pallas_call x1, Pallas kernels, gather(): pl.pallas_call(functools.partial(gather_kernel, chans, walls), out_shape=...  18.4 us
    pallas_call x1, Pallas kernels, hand_back(): pl.pallas_call(functools.partial(return_kernel, chans, walls, tiles), out...  12.4 us

commit v1 on v0

v1 whole, which is shorter than its diff:
```python
import functools
import math

import jax
import jax.numpy as jnp
from jax import lax
from jax.experimental import pallas as pl
from jax.experimental.pallas import tpu as pltpu
from jax.sharding import PartitionSpec as P

NB = 2
R = 4
LANES = 128
ROWS = 64
SHIFT = 6
PIECE = 32
MESH = pl.DeviceIdType.MESH


def wall_cases(wall, walls, flip):
    cases = []
    for s in range(3):
        other = wall + (1 - s if flip else s - 1)
        cases.append((s, other, jnp.logical_and(other >= 0, other < walls)))
    return cases


def gather_kernel(chans, walls, own_ref, ext_ref, send_sem, recv_sem, local_sem):
    chan = lax.axis_index("chan")
    wall = lax.axis_index("wall")
    valid = 1 + (wall > 0).astype(jnp.int32) + (wall < walls - 1).astype(jnp.int32)
    keep = pltpu.make_async_copy(own_ref, ext_ref.at[1], local_sem)
    keep.start()
    barrier = pltpu.get_barrier_semaphore()
    for s, other, there in wall_cases(wall, walls, False):
        @pl.when(there)
        def _(s=s, other=other):
            for k in range(R + 1):
                if k == 0 and s == 1:
                    continue
                pl.semaphore_signal(
                    barrier, inc=1, device_id=(lax.rem(chan + k, chans), other), device_id_type=MESH
                )
    pl.semaphore_wait(barrier, (R + 1) * valid - 1)

    def copy(k, s, other):
        return pltpu.make_async_remote_copy(
            src_ref=own_ref,
            dst_ref=ext_ref.at[k * 3 + s],
            send_sem=send_sem.at[k * 3 + s],
            recv_sem=recv_sem.at[k * 3 + s],
            device_id=(lax.rem(chan + chans - k, chans), other),
            device_id_type=MESH,
        )

    for k in range(R, -1, -1):
        for s, other, there in wall_cases(wall, walls, True):
            if k == 0 and s == 1:
                continue

            @pl.when(there)
            def _(k=k, s=s, other=other):
                copy(k, s, other).start()

    for k in range(R + 1):
        for s, other, there in wall_cases(wall, walls, False):
            if k == 0 and s == 1:
                continue

            @pl.when(there)
            def _(k=k, s=s, other=other):
                copy(k, s, other).wait_recv()

    for k in range(R + 1):
        for s, other, there in wall_cases(wall, walls, True):
            if k == 0 and s == 1:
                continue

            @pl.when(there)
            def _(k=k, s=s, other=other):
                copy(k, s, other).wait_send()
    keep.wait()


def gather(own, chans, walls):
    slots = (R + 1) * 3
    return pl.pallas_call(
        functools.partial(gather_kernel, chans, walls),
        out_shape=jax.ShapeDtypeStruct((slots,) + own.shape, own.dtype),
        in_specs=[pl.BlockSpec(memory_space=pltpu.VMEM)],
        out_specs=pl.BlockSpec(memory_space=pl.ANY),
        scratch_shapes=[
            pltpu.SemaphoreType.DMA((slots,)),
            pltpu.SemaphoreType.DMA((slots,)),
            pltpu.SemaphoreType.DMA,
        ],
        compiler_params=pltpu.CompilerParams(collective_id=0, has_side_effects=True),
    )(own)


def splits(v):
    first = v.astype(jnp.bfloat16).astype(jnp.float32)
    rest = v - first
    second = rest.astype(jnp.bfloat16).astype(jnp.float32)
    third = (rest - second).astype(jnp.bfloat16).astype(jnp.float32)
    return first, second, third


def halves(block, row):
    low = jnp.broadcast_to(block[row : row + 1], block.shape)
    high = jnp.broadcast_to(block[row + 4 : row + 5], block.shape)
    spot = lax.broadcasted_iota(jnp.int32, block.shape, 0)
    return low, high, jnp.where(spot < 4, low, high)


def pair_kernel(
    walls,
    lists_ref,
    counts_ref,
    own_ref,
    ext_ref,
    gained_ref,
    handed_ref,
    afeat,
    wcol,
    bfeat,
    brow,
    gacc,
    hands,
    used,
    blocks_ref,
    queues,
    items,
    sizes,
    sem,
):
    tiles, _, tile_len = own_ref.shape
    slots = ext_ref.shape[0] * 2
    list_len = lists_ref.shape[0] // ((R + 1) * tiles)
    wall = lax.axis_index("wall")
    turned = [
        jnp.transpose((ext_ref[:, half + 3, LANES:] > 0.0).astype(jnp.float32), (1, 0))
        for half in (0, 4)
    ]
    used[...] = jnp.concatenate([turned[0][:1]] + [turned[1][:7]], axis=0).astype(jnp.int32)
    fetch = pltpu.make_async_copy(used, blocks_ref, sem)
    fetch.start()
    spot = lax.broadcasted_iota(jnp.int32, (8, tile_len), 0)
    part = jnp.bitwise_and(spot, 3)
    quarter = 1.0 / R
    base = jnp.where(part == 0, -0.5, jnp.where(part == 3, 0.0, -float(R))) * quarter
    scale = jnp.where(part == 3, 1.0, quarter)

    def own_pair(i, carry):
        block = own_ref[2 * i], own_ref[2 * i + 1]
        block = jnp.concatenate(block, axis=0)
        _, _, s = halves(block, 3)
        place = jnp.where(part == 3, 0.0, block * scale + base)
        square = place * place
        pairsum = square + pltpu.roll(square, 1, 0)
        total = pairsum + pltpu.roll(pairsum, 2, 0)
        full = jnp.where(part == 3, total, place)
        one, two, three = splits(full)
        ones = jnp.where(part == 3, 1.0, 0.0)
        weight = s * s * s
        rest = jnp.zeros((LANES - 80, tile_len), jnp.float32)
        stack = jnp.concatenate(
            [one, one, two, two, one, three, ones, ones, ones, weight, rest], axis=0
        )
        turned = jnp.transpose(stack, (1, 0))
        lane = lax.broadcasted_iota(jnp.int32, turned.shape, 1)
        low = jnp.bitwise_and(lane, 4) == 0
        inside = lane < 72
        for half in range(2):
            t = 2 * i + half
            keep = low if half == 0 else jnp.logical_not(low)
            mine = jnp.where(jnp.logical_and(keep, inside), turned, 0.0)
            other = pltpu.roll(mine, 4 if half == 0 else LANES - 4, 1)
            afeat[half * tiles + t] = mine.astype(jnp.bfloat16)
            afeat[(1 - half) * tiles + t] = other.astype(jnp.bfloat16)
            wcol[t] = jnp.broadcast_to(
                turned[:, 72 + 4 * half : 73 + 4 * half], (tile_len, LANES)
            )
            gacc[t] = jnp.zeros((tile_len, LANES), jnp.float32)
        return carry

    lax.fori_loop(0, tiles // 2, own_pair, 0)
    hands[...] = jnp.zeros_like(hands)

    for k in range(R + 1):
        for slab in range(3):
            edge = wall + slab - 1
            shift = jnp.where(
                part == 0, k * quarter, jnp.where(part == 1, (slab - 1) * 2.0, 0.0)
            )

            def ext_pair(i, carry, k=k, slab=slab, shift=shift):
                at = (k * 3 + slab) * (tiles // 2) + i
                block = ext_ref[at]
                low, high, s = halves(block, 3)
                filled = s > 0.0
                place = block * scale + (base + shift)
                place = jnp.where(jnp.logical_and(part < 3, filled), place, 0.0)
                s = jnp.where(filled, s, 1.0)
                s2 = s * s
                square = place * place
                pairsum = square + pltpu.roll(square, 1, 0)
                total = pairsum + pltpu.roll(pairsum, 2, 0)
                tail = jnp.where(filled, s2 * (total + 0.0001 / (R * R)), 128.0)
                full = jnp.where(part == 3, s2, -2.0 * s2 * place)
                one, two, three = splits(full)
                first, second, third = splits(tail)
                stack = jnp.concatenate(
                    [one, two, one, two, three, one, first, second, third, jnp.zeros_like(one)],
                    axis=0,
                )
                bfeat[at] = stack.astype(jnp.bfloat16)
                for half, root in enumerate((low, high)):
                    root = jnp.where(root > 0.0, root, 1.0)
                    brow[at * 2 + half, :8] = 2.0 * root
                    brow[at * 2 + half, 8:] = 4.0 * root * root * root
                return carry

            @pl.when(jnp.logical_and(edge >= 0, edge < walls))
            def _(ext_pair=ext_pair):
                lax.fori_loop(0, tiles // 2, ext_pair, 0)

    fetch.wait()

    classes = 2 * (tile_len // ROWS)
    room = queues.shape[0] // classes
    low = jnp.where(wall == 0, tiles, 0)
    high = jnp.where(wall == walls - 1, 2 * tiles, 3 * tiles)
    for c in range(classes):
        sizes[c] = 0

    def enlist(t, carry):
        groups = lax.shift_right_logical(counts_ref[t] + (ROWS - 1), SHIFT)
        kind = groups * 2 - 2
        first, second = sizes[kind], sizes[kind + 1]
        base = kind * room
        high_bits = lax.shift_left(t, 16)
        for k in range(R + 1):
            for j in range(list_len):
                tile = lists_ref[(k * tiles + t) * list_len + j]
                at = k * 3 * tiles + tile
                real = jnp.logical_and(tile >= low, tile < high).astype(jnp.int32)
                wide = blocks_ref[jnp.bitwise_and(at, 1), lax.shift_right_logical(at, 1)]
                packed = at + high_bits
                queues[base + first] = packed
                queues[base + room + second] = packed
                both = jnp.bitwise_and(wide, real)
                second = second + both
                first = first + (real - both)
        sizes[kind] = first
        sizes[kind + 1] = second
        return carry

    lax.fori_loop(0, tiles, enlist, 0)
    nothing = (tiles << 16) + slots
    ends = [0]
    for c in reversed(range(classes)):
        size = sizes[c]
        start = ends[-1]

        def move(i, carry, c=c, start=start):
            for d in range(4):
                items[2 * start + 4 * i + d] = queues[c * room + 4 * i + d]
            return carry

        lax.fori_loop(0, lax.shift_right_logical(size + 3, 2), move, 0)
        items[2 * start + size] = nothing
        ends.append(start + lax.shift_right_logical(size + 1, 1))
    for d in range(4):
        items[2 * ends[-1] + d] = nothing

    def body(*accs):
        pieces = tile_len // PIECE
        for ref in accs:
            pltpu.matmul_pop(ref)

        def fields(m):
            packed = items[m]
            at = jnp.bitwise_and(packed, 65535)
            return at, lax.shift_right_logical(packed, 16)

        def push(m, q):
            at, _ = fields(m)
            rhs = jnp.concatenate(
                [
                    bfeat[lax.shift_right_logical(at, 1)],
                    jnp.zeros((256 - 80, tile_len), jnp.bfloat16),
                ],
                axis=0,
            )
            pltpu.matmul_push_rhs(rhs, staging_register=0, mxu_index=q)

        def feed(which, q, p):
            lhs = afeat[which, p * PIECE : (p + 1) * PIECE]
            lhs = jnp.concatenate([lhs, jnp.zeros((PIECE, 256 - LANES), jnp.bfloat16)], axis=1)
            pltpu.matmul_acc_lhs(
                accs[q * pieces + p], lhs, load_staged_rhs=0 if p == 0 else None
            )

        def which_of(m):
            at, t = fields(m)
            return jnp.bitwise_and(at, 1) * tiles + t

        def run(j, carry, groups, width):
            now = [fields(2 * j + q) for q in range(2)]
            then = [which_of(2 * j + 2 + q) for q in range(2)]
            rows = [
                [brow[at, r * 8 : r * 8 + 8, h * LANES : (h + 1) * LANES] for r in range(2) for h in range(width)]
                for at, _ in now
            ]
            sums = [[None] * width for _ in now]
            for p in range(groups * ROWS // PIECE):
                for q, (at, t) in enumerate(now):
                    u = pltpu.matmul_pop(accs[q * pieces + p])
                    feed(then[q], q, p)
                    if p == 0:
                        push(2 * j + 4 + q, q)
                    for r in range(0, PIECE, 8):
                        here = pl.ds(p * PIECE + r, 8)
                        aw = wcol[t, here, :]
                        total = None
                        for h in range(width):
                            v = u[r : r + 8, h * LANES : (h + 1) * LANES]
                            o = jnp.maximum(rows[q][h] - v * lax.rsqrt(v), 0.0)
                            w = jnp.minimum(o * o * o, rows[q][width + h] - (v * o) * 3.0)
                            total = w if total is None else total + w
                            back = w * aw
                            sums[q][h] = back if sums[q][h] is None else sums[q][h] + back
                        gacc[t, here, :] += total
            for q, (at, t) in enumerate(now):
                for h in range(width):
                    hands[at, :, h * LANES : (h + 1) * LANES] += sums[q][h]
            return carry

        for q in range(2):
            push(q, q)
        for q in range(2):
            for p in range(pieces):
                feed(which_of(q), q, p)
        for q in range(2):
            push(2 + q, q)
        for c in range(classes):
            kind = classes - 1 - c
            lax.fori_loop(
                ends[c],
                ends[c + 1],
                functools.partial(run, groups=kind // 2 + 1, width=1 + kind % 2),
                0,
            )
        for q in range(2):
            for p in range(pieces):
                feed(which_of(q), q, p)
        for ref in accs:
            pltpu.matmul_pop(ref)

    pl.run_scoped(
        body,
        *[pltpu.ACC(q)((PIECE, 256), jnp.float32) for q in range(2) for _ in range(tile_len // PIECE)],
    )
    for t in range(tiles):
        gained_ref[t] = jnp.sum(jnp.sum(
            jnp.transpose(gacc[t], (1, 0)).reshape(LANES // 8, 8, tile_len), axis=0
        ), axis=0)
    handed_ref[...] = jnp.sum(hands[:slots], axis=1)


def pairs(lists, counts, own, ext, walls):
    tiles, _, tile_len = own.shape
    smem = pl.BlockSpec(memory_space=pltpu.SMEM)
    vmem = pl.BlockSpec(memory_space=pltpu.VMEM)
    slots = ext.shape[0] * 2
    return pl.pallas_call(
        functools.partial(pair_kernel, walls),
        out_shape=(
            jax.ShapeDtypeStruct((tiles, tile_len), jnp.float32),
            jax.ShapeDtypeStruct((slots, tile_len), jnp.float32),
        ),
        in_specs=[smem, smem, vmem, vmem],
        out_specs=(vmem, vmem),
        scratch_shapes=[
            pltpu.VMEM((2 * tiles, tile_len, LANES), jnp.bfloat16),
            pltpu.VMEM((tiles + 1, tile_len, LANES), jnp.float32),
            pltpu.VMEM((slots // 2 + 1, 80, tile_len), jnp.bfloat16),
            pltpu.VMEM((slots + 1, 16, tile_len), jnp.float32),
            pltpu.VMEM((tiles + 1, tile_len, LANES), jnp.float32),
            pltpu.VMEM((slots + 1, 8, tile_len), jnp.float32),
            pltpu.VMEM((8, slots // 2), jnp.int32),
            pltpu.SMEM((8, slots // 2), jnp.int32),
            pltpu.SMEM((2 * (tile_len // ROWS) * (lists.shape[0] + 8),), jnp.int32),
            pltpu.SMEM((lists.shape[0] + 32,), jnp.int32),
            pltpu.SMEM((2 * (tile_len // ROWS),), jnp.int32),
            pltpu.SemaphoreType.DMA,
        ],
    )(lists, counts, own, ext)


def return_kernel(
    chans, walls, tiles, gained_ref, handed_ref, over_ref, out_ref, held, send_sem, recv_sem
):
    chan = lax.axis_index("chan")
    wall = lax.axis_index("wall")
    valid = 1 + (wall > 0).astype(jnp.int32) + (wall < walls - 1).astype(jnp.int32)
    barrier = pltpu.get_barrier_semaphore()
    for s, other, there in wall_cases(wall, walls, True):
        @pl.when(there)
        def _(s=s, other=other):
            for k in range(1, R + 1):
                pl.semaphore_signal(
                    barrier,
                    inc=1,
                    device_id=(lax.rem(chan + chans - k, chans), other),
                    device_id_type=MESH,
                )
    pl.semaphore_wait(barrier, R * valid)

    def copy(k, s, other):
        slot = (k - 1) * 3 + s
        return pltpu.make_async_remote_copy(
            src_ref=handed_ref.at[pl.ds((k * 3 + s) * tiles, tiles)],
            dst_ref=held.at[slot],
            send_sem=send_sem.at[slot],
            recv_sem=recv_sem.at[slot],
            device_id=(lax.rem(chan + k, chans), other),
            device_id_type=MESH,
        )

    for k in range(R, 0, -1):
        for s, other, there in wall_cases(wall, walls, False):
            @pl.when(there)
            def _(k=k, s=s, other=other):
                copy(k, s, other).start()

    out_ref[...] = gained_ref[...]
    for k in range(1, R + 1):
        for s, other, there in wall_cases(wall, walls, True):
            @pl.when(there)
            def _(k=k, s=s, other=other):
                copy(k, s, other).wait_recv()
                out_ref[...] += held[(k - 1) * 3 + s] * over_ref[...]

    for k in range(1, R + 1):
        for s, other, there in wall_cases(wall, walls, False):
            @pl.when(there)
            def _(k=k, s=s, other=other):
                copy(k, s, other).wait_send()


def hand_back(gained, handed, over, chans, walls):
    tiles, tile_len = gained.shape
    vmem = pl.BlockSpec(memory_space=pltpu.VMEM)
    return pl.pallas_call(
        functools.partial(return_kernel, chans, walls, tiles),
        out_shape=jax.ShapeDtypeStruct(gained.shape, gained.dtype),
        in_specs=[vmem, vmem, vmem],
        out_specs=vmem,
        scratch_shapes=[
            pltpu.VMEM((R * 3, tiles, tile_len), jnp.float32),
            pltpu.SemaphoreType.DMA((R * 3,)),
            pltpu.SemaphoreType.DMA((R * 3,)),
        ],
        compiler_params=pltpu.CompilerParams(collective_id=1, has_side_effects=True),
    )(gained, handed, over)


def on_device(chans, walls, coords, masses, counts, lists):
    tiles = counts.shape[2]
    tile_len = masses.shape[2] // tiles
    slots = jnp.arange(tile_len, dtype=jnp.int32)
    filled = (slots[None, :] < counts[0, 0][:, None]).astype(jnp.float32)
    weighted = masses.reshape(tiles, tile_len)
    root = jnp.exp(jnp.log(weighted) * (1.0 / 3.0))
    root = root - (root * root * root - weighted) / (3.0 * root * root)
    own = jnp.concatenate([coords.reshape(3, tiles, tile_len), (root * filled)[None]], axis=0)
    own = jnp.moveaxis(own, 0, 1)
    ext = gather(own.reshape(tiles // 2, 8, tile_len), chans, walls)
    gained, handed = pairs(
        lists.reshape(-1), counts.reshape(-1), own, ext.reshape(-1, 8, tile_len), walls
    )
    over = filled / weighted
    total = hand_back(gained, handed, over, chans, walls)
    scale = 1.0 / (4.0 * math.pi * NB * tile_len)
    return (total * filled * scale).reshape(1, 1, -1)


def solution(mesh):
    placed = (
        P(None, "chan", "wall", None),
        P("chan", "wall", None),
        P("chan", "wall", None),
        P("chan", "wall", None, None, None),
    )
    body = functools.partial(on_device, mesh.shape["chan"], mesh.shape["wall"])
    return jax.shard_map(
        body, mesh=mesh, in_specs=placed, out_specs=P("chan", "wall", None), check_vma=False
    )
```

time: 71.3 us -> 58.3 us (0.82); the launches traced: 70.5 us -> 58.4 us
  Pallas kernels: 66 us -> 50.6 us
  local copies, waits for them, and re-layouts: 2.12 us -> 3.89 us
  other arithmetic: 2.39 us -> 3.83 us
    pallas_call x1, Pallas kernels: 35.1 us -> 19.5 us  [pairs(): pl.pallas_call(functools.partial(pair_kernel, walls), out_shape=(jax.Shap...]
    unnamed x1 -> x2, other arithmetic: 0.13 us -> 1.53 us
    unnamed x9 -> x12, local copies, waits for them, and re-layouts: 0.78 us -> 1.92 us
where the time goes in v1:
time: 58.3 us; the launch traced here: 58.4 us
  Pallas kernels  50.6 us (87%)
  local copies, waits for them, and re-layouts  3.89 us (7%)
  other arithmetic  3.83 us (7%)
    pallas_call x1, Pallas kernels, pairs(): pl.pallas_call(functools.partial(pair_kernel, walls), out_shape=(jax.Shap...  19.5 us
    pallas_call x1, Pallas kernels, gather(): pl.pallas_call(functools.partial(gather_kernel, chans, walls), out_shape=...  18.4 us
    pallas_call x1, Pallas kernels, hand_back(): pl.pallas_call(functools.partial(return_kernel, chans, walls, tiles), out...  12.7 us
    unnamed x12, local copies, waits for them, and re-layouts  1.92 us
    unnamed x2, other arithmetic  1.53 us

profile of v1, /device:TPU:0, one launch (start us, length us, event | category | flops | bytes accessed | tf_op | source)
XLA Modules:
  0.0 58.4 jit_solution(13991925778558691442)
XLA Ops:
  0.0 0.0 copy-start.2
  0.0 0.7 %copy-done.2 = s32[1,1,16]{2,1,0:T(1,128)S(1)} copy-done((s32[1,1,16]{2,1,0:T(1,128)S(1)}, s32[1,1,16]{2,1,0:T(1,128)}, u32[]{:S(2)}) %copy-start.2) | copy-done | bytes 88
  0.7 0.8 %compare_select_fusion = f32[1,16,256]{2,0,1:T(1,128)S(1)} fusion(f32[1,16,256]{2,0,1:T(1,128)} %bitcast.10, s32[16]{0:T(128)S(1)} %bitcast.12), kind=kLoop, calls=%fused_computation.1 | loop fusion | flops 40960 | bytes 32832 | tf_op jit(solution)/shard_map/mul | solution.py:478
  1.5 0.9 %reduce = f32[3,4096]{1,0:T(4,128)S(1)} reduce(f32[3,1,1,4096]{3,2,1,0:T(1,128)} %param.4, f32[]{:T(128)} %constant.13), dimensions={1,2}, to_apply=%param.4.reduce_sub_computation | reduce | bytes 98308 | tf_op args[0]
  2.4 0.0 copy-start
  2.4 0.7 %reshape.109.own_ref = f32[8,8,256]{2,1,0:T(8,128)} reshape(f32[16,4,256]{2,1,0:T(4,128)S(1)} %maximum_bitcast_fusion.own_ref) | data formatting | bytes 131072 | tf_op jit(solution)/shard_map/reshape | solution.py:480
  3.1 0.0 copy-done
  3.1 0.0 copy-start.4
  3.1 18.4 %shard_map.46 = f32[15,8,8,256]{3,2,1,0:T(8,128)} custom-call(f32[8,8,256]{2,1,0:T(8,128)} %reshape.109.own_ref), custom_call_target="tpu_custom_call" | custom-call | tf_op jit(solution)/shard_map/pallas_call | solution.py:87
  21.6 0.0 copy-done.4
  21.6 0.1 copy.7
  21.7 0.7 %reshape.106.lists_ref = s32[160]{0:T(256)} reshape(s32[1,1,5,16,2]{4,3,2,1,0:T(8,128)S(1)} %copy.7) | data formatting | bytes 1280 | tf_op jit(solution)/shard_map/reshape | solution.py:482
  22.4 0.0 copy-start.1
  22.4 19.5 %shard_map.47 = (f32[16,256]{1,0:T(8,128)}, f32[240,256]{1,0:T(8,128)}) custom-call(s32[160]{0:T(256)} %reshape.106.lists_ref, s32[16]{0:T(128)} %bitcast.11, f32[16,4,256]{2,1,0:T(4,128)} %copy-done, f32[120,8,256]{2,1,0:T(8,128)} %bitcast.8), custom_call_target="tpu_custom_call" | custom-call | tf_op jit(solution)/shard_map/pallas_call | solution.py:377
  41.8 0.5 broadcast.53
  42.3 0.0 copy-done.1
  42.3 0.6 %reduce.4 = f32[4096]{0:T(1024)S(1)} reduce(f32[1,1,4096]{2,1,0:T(1,128)S(1)} %copy-done.1, f32[]{:T(128)} %broadcast.53), dimensions={0,1}, to_apply=%param.5.reduce_sub_computation.3 | reduce | bytes 32772 | tf_op args[1]
  42.9 0.0 copy-start.3
  43.0 0.6 %copy-done.3 = s32[1,1,16]{2,1,0:T(1,128)S(1)} copy-done((s32[1,1,16]{2,1,0:T(1,128)S(1)}, s32[1,1,16]{2,1,0:T(1,128)}, u32[]{:S(2)}) %copy-start.3) | copy-done | bytes 88
  43.6 0.7 %convert_divide_fusion.over_ref = f32[16,256]{1,0:T(8,128)} fusion(f32[16,256]{1,0:T(8,128)S(1)} %reshape.111, s32[16]{0:T(128)S(1)} %bitcast.13), kind=kLoop, calls=%fused_computation.8 | loop fusion | flops 12288 | bytes 32832 | tf_op jit(solution)/shard_map/div | solution.py:484
  44.3 12.7 %shard_map.48 = f32[16,256]{1,0:T(8,128)} custom-call(f32[16,256]{1,0:T(8,128)} %get-tuple-element.7.gained_ref, f32[240,256]{1,0:T(8,128)} %get-tuple-element.8.handed_ref, f32[16,256]{1,0:T(8,128)} %convert_divide_fusion.over_ref), custom_call_target="tpu_custom_call" | custom-call | tf_op jit(solution)/shard_map/pallas_call | solution.py:456
  56.9 0.8 %select_multiply_fusion = f32[16,256]{1,0:T(8,128)S(1)} fusion(f32[16,256]{1,0:T(8,128)} %shard_map.48, s32[16]{0:T(128)S(1)} %bitcast.14), kind=kLoop, calls=%fused_computation.7 | loop fusion | flops 12288 | bytes 32832 | tf_op jit(solution)/shard_map/mul | solution.py:487
  57.7 0.6 %reshape.112 = f32[1,1,4096]{2,1,0:T(1,128)} reshape(f32[16,256]{1,0:T(8,128)S(1)} %select_multiply_fusion) | data formatting | bytes 32768 | tf_op jit(solution)/shard_map/reshape | solution.py:487
  (2 shorter events, 0.0 us)
Async XLA Ops:
  0.0 0.7 %copy-start.2 = (s32[1,1,16]{2,1,0:T(1,128)S(1)}, s32[1,1,16]{2,1,0:T(1,128)}, u32[]{:S(2)}) copy-start(s32[1,1,16]{2,1,0:T(1,128)} %param.6) | copy-start | bytes 196
  2.4 0.7 %copy-start = (f32[16,4,256]{2,1,0:T(4,128)}, f32[16,4,256]{2,1,0:T(4,128)S(1)}, u32[]{:S(2)}) copy-start(f32[16,4,256]{2,1,0:T(4,128)S(1)} %maximum_bitcast_fusion.own_ref) | copy-start | bytes 196612
  3.1 18.5 %copy-start.4 = (s32[1,1,5,16,2]{3,4,2,1,0:T(2,128)S(1)}, s32[1,1,5,16,2]{3,4,2,1,0:T(2,128)}, u32[]{:S(2)}) copy-start(s32[1,1,5,16,2]{3,4,2,1,0:T(2,128)} %param.7) | copy-start | bytes 1924
  22.4 20.0 %copy-start.1 = (f32[1,1,4096]{2,1,0:T(1,128)S(1)}, f32[1,1,4096]{2,1,0:T(1,128)}, u32[]{:S(2)}) copy-start(f32[1,1,4096]{2,1,0:T(1,128)} %param.5) | copy-start | bytes 49156
  42.9 0.7 %copy-start.3 = (s32[1,1,16]{2,1,0:T(1,128)S(1)}, s32[1,1,16]{2,1,0:T(1,128)}, u32[]{:S(2)}) copy-start(s32[1,1,16]{2,1,0:T(1,128)} %param.6) | copy-start | bytes 196

commit v2 on v1

--- a/solution.py
+++ b/solution.py
@@ -25,23 +25,63 @@
     return cases
 
 
-def gather_kernel(chans, walls, own_ref, ext_ref, send_sem, recv_sem, local_sem):
+def gather_kernel(
+    chans,
+    walls,
+    coords_ref,
+    masses_ref,
+    counts_ref,
+    ext_ref,
+    over_ref,
+    own_ref,
+    send_sem,
+    recv_sem,
+    pass_sem,
+    local_sem,
+):
     chan = lax.axis_index("chan")
     wall = lax.axis_index("wall")
+    odd = lax.rem(chan, 2)
+    twin = chan + 1 - 2 * odd
     valid = 1 + (wall > 0).astype(jnp.int32) + (wall < walls - 1).astype(jnp.int32)
-    keep = pltpu.make_async_copy(own_ref, ext_ref.at[1], local_sem)
-    keep.start()
     barrier = pltpu.get_barrier_semaphore()
     for s, other, there in wall_cases(wall, walls, False):
         @pl.when(there)
         def _(s=s, other=other):
-            for k in range(R + 1):
+            for k in (0, 2, 4):
                 if k == 0 and s == 1:
                     continue
                 pl.semaphore_signal(
                     barrier, inc=1, device_id=(lax.rem(chan + k, chans), other), device_id_type=MESH
                 )
-    pl.semaphore_wait(barrier, (R + 1) * valid - 1)
+    pl.semaphore_signal(barrier, inc=1, device_id=(twin, wall), device_id_type=MESH)
+
+    tiles, tile_len = over_ref.shape[1:]
+    parts = tile_len // LANES
+    height = tiles * parts
+
+    def load(ref, base):
+        return jnp.concatenate(
+            [ref[pl.ds(base + h, tiles, stride=parts), :] for h in range(parts)], axis=1
+        )
+
+    spot = lax.broadcasted_iota(jnp.int32, (tiles, tile_len), 0)
+    slot = lax.broadcasted_iota(jnp.int32, (tiles, tile_len), 1)
+    limit = jnp.zeros((tiles, tile_len), jnp.int32)
+    for t in range(tiles):
+        limit = jnp.where(spot == t, counts_ref[t], limit)
+    filled = slot < limit
+    mass = load(masses_ref, 0)
+    root = jnp.exp(jnp.log(mass) * (1.0 / 3.0))
+    root = root - (root * root * root - mass) / (3.0 * root * root)
+    over_ref[0] = jnp.where(filled, 1.0, 0.0)
+    over_ref[1] = jnp.where(filled, 1.0 / mass, 0.0)
+    fields = [load(coords_ref, i * height) for i in range(3)] + [jnp.where(filled, root, 0.0)]
+    for i, field in enumerate(fields):
+        for h in range(parts):
+            own_ref[h, pl.ds(i, tiles, stride=4), :] = field[:, h * LANES : (h + 1) * LANES]
+
+    pl.semaphore_wait(barrier, 3 * valid)
 
     def copy(k, s, other):
         return pltpu.make_async_remote_copy(
@@ -53,49 +93,88 @@
             device_id_type=MESH,
         )
 
-    for k in range(R, -1, -1):
-        for s, other, there in wall_cases(wall, walls, True):
-            if k == 0 and s == 1:
-                continue
-
-            @pl.when(there)
-            def _(k=k, s=s, other=other):
-                copy(k, s, other).start()
-
-    for k in range(R + 1):
-        for s, other, there in wall_cases(wall, walls, False):
-            if k == 0 and s == 1:
-                continue
-
-            @pl.when(there)
-            def _(k=k, s=s, other=other):
-                copy(k, s, other).wait_recv()
-
-    for k in range(R + 1):
-        for s, other, there in wall_cases(wall, walls, True):
-            if k == 0 and s == 1:
-                continue
-
-            @pl.when(there)
-            def _(k=k, s=s, other=other):
-                copy(k, s, other).wait_send()
+    def relay(k, s, own=False):
+        into = k - 1 + 2 * odd
+        return pltpu.make_async_remote_copy(
+            src_ref=own_ref if own else ext_ref.at[k * 3 + s],
+            dst_ref=ext_ref.at[into * 3 + s],
+            send_sem=pass_sem.at[into * 3 + s],
+            recv_sem=recv_sem.at[into * 3 + s],
+            device_id=(twin, wall),
+            device_id_type=MESH,
+        )
+
+    def each(flip, ks, order, run):
+        cases = wall_cases(wall, walls, flip)
+        for s in order:
+            _, other, there = cases[s]
+            for k in ks:
+                if k == 0 and s == 1:
+                    continue
+
+                @pl.when(there)
+                def _(k=k, s=s, other=other):
+                    run(k, s, other)
+
+    each(True, (2, 4), (1, 0, 2), lambda k, s, other: copy(k, s, other).start())
+    each(True, (0,), (0, 2), lambda k, s, other: copy(k, s, other).start())
+    keep = pltpu.make_async_copy(own_ref, ext_ref.at[1], local_sem)
+    keep.start()
+
+    def forward(k, s, other):
+        copy(k, s, other).wait_recv()
+        relay(k, s).start()
+
+    @pl.when(odd == 0)
+    def _():
+        each(False, (2, 4), (1, 0, 2), forward)
+        each(False, (0,), (0, 2), lambda k, s, other: copy(k, s, other).wait_recv())
+
+    @pl.when(odd == 1)
+    def _():
+        relay(0, 1, True).start()
+        each(False, (2,), (1,), forward)
+        each(False, (0, 2), (0, 2), forward)
+        each(False, (4,), (1, 0, 2), lambda k, s, other: copy(k, s, other).wait_recv())
+
+    each(False, (1, 3), (1, 0, 2), lambda k, s, other: copy(k, s, other).wait_recv())
+    each(True, (0, 2, 4), (0, 1, 2), lambda k, s, other: copy(k, s, other).wait_send())
+
+    @pl.when(odd == 0)
+    def _():
+        each(False, (2, 4), (0, 1, 2), lambda k, s, other: relay(k, s).wait_send())
+
+    @pl.when(odd == 1)
+    def _():
+        relay(0, 1, True).wait_send()
+        each(False, (0, 2), (0, 1, 2), lambda k, s, other: relay(k, s).wait_send())
+
     keep.wait()
 
 
-def gather(own, chans, walls):
+def gather(coords, masses, counts, chans, walls):
     slots = (R + 1) * 3
+    tiles = counts.shape[0]
+    tile_len = masses.shape[0] * LANES // tiles
+    vmem = pl.BlockSpec(memory_space=pltpu.VMEM)
+    block = (tile_len // LANES, 4 * tiles, LANES)
     return pl.pallas_call(
         functools.partial(gather_kernel, chans, walls),
-        out_shape=jax.ShapeDtypeStruct((slots,) + own.shape, own.dtype),
-        in_specs=[pl.BlockSpec(memory_space=pltpu.VMEM)],
-        out_specs=pl.BlockSpec(memory_space=pl.ANY),
+        out_shape=(
+            jax.ShapeDtypeStruct((slots,) + block, jnp.float32),
+            jax.ShapeDtypeStruct((2, tiles, tile_len), jnp.float32),
+        ),
+        in_specs=[vmem, vmem, pl.BlockSpec(memory_space=pltpu.SMEM)],
+        out_specs=(pl.BlockSpec(memory_space=pl.ANY), vmem),
         scratch_shapes=[
+            pltpu.VMEM(block, jnp.float32),
+            pltpu.SemaphoreType.DMA((slots,)),
             pltpu.SemaphoreType.DMA((slots,)),
             pltpu.SemaphoreType.DMA((slots,)),
             pltpu.SemaphoreType.DMA,
         ],
         compiler_params=pltpu.CompilerParams(collective_id=0, has_side_effects=True),
-    )(own)
+    )(coords, masses, counts)
 
 
 def splits(v):
@@ -117,8 +196,7 @@
     walls,
     lists_ref,
     counts_ref,
-    own_ref,
-    ext_ref,
+    far_ref,
     gained_ref,
     handed_ref,
     afeat,
@@ -132,19 +210,38 @@
     queues,
     items,
     sizes,
+    ext_ref,
+    marks,
     sem,
+    load_sem,
 ):
-    tiles, _, tile_len = own_ref.shape
-    slots = ext_ref.shape[0] * 2
-    list_len = lists_ref.shape[0] // ((R + 1) * tiles)
+    tiles, tile_len = gained_ref.shape
+    slots = handed_ref.shape[0]
+    parts = tile_len // LANES
+    list_len = lists_ref.shape[1]
     wall = lax.axis_index("wall")
-    turned = [
-        jnp.transpose((ext_ref[:, half + 3, LANES:] > 0.0).astype(jnp.float32), (1, 0))
-        for half in (0, 4)
-    ]
-    used[...] = jnp.concatenate([turned[0][:1]] + [turned[1][:7]], axis=0).astype(jnp.int32)
-    fetch = pltpu.make_async_copy(used, blocks_ref, sem)
-    fetch.start()
+
+    def bring(at):
+        return pltpu.make_async_copy(far_ref.at[at], ext_ref.at[at], load_sem.at[at])
+
+    def sides(run):
+        for slab in range(3):
+            edge = wall + slab - 1
+
+            @pl.when(jnp.logical_and(edge >= 0, edge < walls))
+            def _(slab=slab):
+                for k in range(R + 1):
+                    if k > 0 or slab != 1:
+                        run(k * 3 + slab)
+
+    bring(1).start()
+    sides(lambda at: bring(at).start())
+    bring(1).wait()
+
+    def block_of(slab, i):
+        rows = pl.ds(pl.multiple_of(i * 8, 8), 8)
+        return jnp.concatenate([ext_ref[slab, h, rows, :] for h in range(parts)], axis=1)
+
     spot = lax.broadcasted_iota(jnp.int32, (8, tile_len), 0)
     part = jnp.bitwise_and(spot, 3)
     quarter = 1.0 / R
@@ -152,8 +249,7 @@
     scale = jnp.where(part == 3, 1.0, quarter)
 
     def own_pair(i, carry):
-        block = own_ref[2 * i], own_ref[2 * i + 1]
-        block = jnp.concatenate(block, axis=0)
+        block = block_of(1, i)
         _, _, s = halves(block, 3)
         place = jnp.where(part == 3, 0.0, block * scale + base)
         square = place * place
@@ -185,6 +281,16 @@
         return carry
 
     lax.fori_loop(0, tiles // 2, own_pair, 0)
+    sides(lambda at: bring(at).wait())
+    for half in range(2):
+        for at in range(ext_ref.shape[0]):
+            marks[half, at * (tiles // 2) : (at + 1) * (tiles // 2), :] = ext_ref[
+                at, 1, pl.ds(half * 4 + 3, tiles // 2, stride=8), :
+            ]
+    turned = [jnp.transpose((marks[half] > 0.0).astype(jnp.float32), (1, 0)) for half in range(2)]
+    used[...] = jnp.concatenate([turned[0][:1], turned[1][:7]], axis=0).astype(jnp.int32)
+    fetch = pltpu.make_async_copy(used, blocks_ref, sem)
+    fetch.start()
     hands[...] = jnp.zeros_like(hands)
 
     for k in range(R + 1):
@@ -196,7 +302,7 @@
 
             def ext_pair(i, carry, k=k, slab=slab, shift=shift):
                 at = (k * 3 + slab) * (tiles // 2) + i
-                block = ext_ref[at]
+                block = block_of(k * 3 + slab, i)
                 low, high, s = halves(block, 3)
                 filled = s > 0.0
                 place = block * scale + (base + shift)
@@ -242,7 +348,7 @@
         high_bits = lax.shift_left(t, 16)
         for k in range(R + 1):
             for j in range(list_len):
-                tile = lists_ref[(k * tiles + t) * list_len + j]
+                tile = lists_ref[k, j, t]
                 at = k * 3 * tiles + tile
                 real = jnp.logical_and(tile >= low, tile < high).astype(jnp.int32)
                 wide = blocks_ref[jnp.bitwise_and(at, 1), lax.shift_right_logical(at, 1)]
@@ -369,18 +475,20 @@
     handed_ref[...] = jnp.sum(hands[:slots], axis=1)
 
 
-def pairs(lists, counts, own, ext, walls):
-    tiles, _, tile_len = own.shape
+def pairs(lists, counts, ext, walls):
+    tiles = counts.shape[0]
+    tile_len = ext.shape[1] * LANES
     smem = pl.BlockSpec(memory_space=pltpu.SMEM)
     vmem = pl.BlockSpec(memory_space=pltpu.VMEM)
-    slots = ext.shape[0] * 2
+    slots = ext.shape[0] * tiles
+    entries = math.prod(lists.shape)
     return pl.pallas_call(
         functools.partial(pair_kernel, walls),
         out_shape=(
             jax.ShapeDtypeStruct((tiles, tile_len), jnp.float32),
             jax.ShapeDtypeStruct((slots, tile_len), jnp.float32),
         ),
-        in_specs=[smem, smem, vmem, vmem],
+        in_specs=[smem, smem, pl.BlockSpec(memory_space=pl.ANY)],
         out_specs=(vmem, vmem),
         scratch_shapes=[
             pltpu.VMEM((2 * tiles, tile_len, LANES), jnp.bfloat16),
@@ -391,16 +499,19 @@
             pltpu.VMEM((slots + 1, 8, tile_len), jnp.float32),
             pltpu.VMEM((8, slots // 2), jnp.int32),
             pltpu.SMEM((8, slots // 2), jnp.int32),
-            pltpu.SMEM((2 * (tile_len // ROWS) * (lists.shape[0] + 8),), jnp.int32),
-            pltpu.SMEM((lists.shape[0] + 32,), jnp.int32),
+            pltpu.SMEM((2 * (tile_len // ROWS) * (entries + 8),), jnp.int32),
+            pltpu.SMEM((entries + 32,), jnp.int32),
             pltpu.SMEM((2 * (tile_len // ROWS),), jnp.int32),
+            pltpu.VMEM(ext.shape, jnp.float32),
+            pltpu.VMEM((2, slots // 2, LANES), jnp.float32),
             pltpu.SemaphoreType.DMA,
+            pltpu.SemaphoreType.DMA((ext.shape[0],)),
         ],
-    )(lists, counts, own, ext)
+    )(lists, counts, ext)
 
 
 def return_kernel(
-    chans, walls, tiles, gained_ref, handed_ref, over_ref, out_ref, held, send_sem, recv_sem
+    chans, walls, tiles, gained_ref, handed_ref, over_ref, out_ref, held, hold, send_sem, recv_sem
 ):
     chan = lax.axis_index("chan")
     wall = lax.axis_index("wall")
@@ -435,14 +546,20 @@
             def _(k=k, s=s, other=other):
                 copy(k, s, other).start()
 
-    out_ref[...] = gained_ref[...]
+    total = gained_ref[...]
+    scale = over_ref[0]
+    back = over_ref[1]
+    hold[...] = total * scale
     for k in range(1, R + 1):
         for s, other, there in wall_cases(wall, walls, True):
             @pl.when(there)
             def _(k=k, s=s, other=other):
                 copy(k, s, other).wait_recv()
-                out_ref[...] += held[(k - 1) * 3 + s] * over_ref[...]
-
+                hold[...] += held[(k - 1) * 3 + s] * back
+
+    parts = hold.shape[1] // LANES
+    for h in range(parts):
+        out_ref[pl.ds(h, tiles, stride=parts), :] = hold[:, h * LANES : (h + 1) * LANES]
     for k in range(1, R + 1):
         for s, other, there in wall_cases(wall, walls, False):
             @pl.when(there)
@@ -455,11 +572,12 @@
     vmem = pl.BlockSpec(memory_space=pltpu.VMEM)
     return pl.pallas_call(
         functools.partial(return_kernel, chans, walls, tiles),
-        out_shape=jax.ShapeDtypeStruct(gained.shape, gained.dtype),
+        out_shape=jax.ShapeDtypeStruct((tiles * tile_len // LANES, LANES), gained.dtype),
         in_specs=[vmem, vmem, vmem],
         out_specs=vmem,
         scratch_shapes=[
             pltpu.VMEM((R * 3, tiles, tile_len), jnp.float32),
+            pltpu.VMEM((tiles, tile_len), jnp.float32),
             pltpu.SemaphoreType.DMA((R * 3,)),
             pltpu.SemaphoreType.DMA((R * 3,)),
         ],
@@ -470,21 +588,15 @@
 def on_device(chans, walls, coords, masses, counts, lists):
     tiles = counts.shape[2]
     tile_len = masses.shape[2] // tiles
-    slots = jnp.arange(tile_len, dtype=jnp.int32)
-    filled = (slots[None, :] < counts[0, 0][:, None]).astype(jnp.float32)
-    weighted = masses.reshape(tiles, tile_len)
-    root = jnp.exp(jnp.log(weighted) * (1.0 / 3.0))
-    root = root - (root * root * root - weighted) / (3.0 * root * root)
-    own = jnp.concatenate([coords.reshape(3, tiles, tile_len), (root * filled)[None]], axis=0)
-    own = jnp.moveaxis(own, 0, 1)
-    ext = gather(own.reshape(tiles // 2, 8, tile_len), chans, walls)
-    gained, handed = pairs(
-        lists.reshape(-1), counts.reshape(-1), own, ext.reshape(-1, 8, tile_len), walls
+    scale = 1.0 / (4.0 * math.pi * NB * tile_len)
+    counts = counts.reshape(-1)
+    ext, over = gather(
+        coords.reshape(-1, LANES), masses.reshape(-1, LANES), counts, chans, walls
     )
-    over = filled / weighted
+    lists = jnp.swapaxes(lists.reshape(lists.shape[2:]), 1, 2)
+    gained, handed = pairs(lists, counts, ext, walls)
     total = hand_back(gained, handed, over, chans, walls)
-    scale = 1.0 / (4.0 * math.pi * NB * tile_len)
-    return (total * filled * scale).reshape(1, 1, -1)
+    return total.reshape(1, 1, -1) * scale
 
 
 def solution(mesh):

time: 58.3 us -> 48.8 us (0.84); the launches traced: 58.4 us -> 48.1 us
  Pallas kernels: 50.6 us -> 46.7 us
  local copies, waits for them, and re-layouts: 3.89 us -> 0 us
  other arithmetic: 3.83 us -> 1.33 us
    pallas_call x1, Pallas kernels: 18.4 us -> 14.7 us  [gather(): pl.pallas_call(functools.partial(gather_kernel, chans, walls), out_shape=...]
    reshape x4 -> x0, local copies, waits for them, and re-layouts: 1.97 us -> none  [the longest x1 0.68 us: on_device(): lists.reshape(-1)]
    pallas_call x1, Pallas kernels: 12.7 us -> 10.7 us  [hand_back(): pl.pallas_call(functools.partial(return_kernel, chans, walls, tiles), out...]
    unnamed x12 -> x0, local copies, waits for them, and re-layouts: 1.92 us -> none
    pallas_call x1, Pallas kernels: 19.5 us -> 21.3 us  [pairs(): pl.pallas_call(functools.partial(pair_kernel, walls), out_shape=(jax.Shap...]
    unnamed x2 -> x0, other arithmetic: 1.53 us -> none
    div x1 -> x0, other arithmetic: 0.67 us -> none  [on_device(): over = filled / weighted]
    mul x2 -> x1, other arithmetic: 1.59 us -> 1.33 us  [on_device(): return total.reshape(1, 1, -1) * scale]
where the time goes in v2:
time: 48.8 us; the launch traced here: 48.1 us
  Pallas kernels  46.7 us (96%)
  other arithmetic  1.33 us (3%)
    pallas_call x1, Pallas kernels, pairs(): pl.pallas_call(functools.partial(pair_kernel, walls), out_shape=(jax.Shap...  21.3 us
    pallas_call x1, Pallas kernels, gather(): pl.pallas_call(functools.partial(gather_kernel, chans, walls), out_shape=...  14.7 us
    pallas_call x1, Pallas kernels, hand_back(): pl.pallas_call(functools.partial(return_kernel, chans, walls, tiles), out...  10.7 us
    mul x1, other arithmetic, on_device(): return total.reshape(1, 1, -1) * scale  1.33 us

profile of v2, /device:TPU:0, one launch (start us, length us, event | category | flops | bytes accessed | tf_op | source)
XLA Modules:
  0.0 48.1 jit_solution(10997830546015469714)
XLA Ops:
  0.0 14.7 %shard_map.46 = (f32[15,2,64,128]{3,2,1,0:T(8,128)}, f32[2,16,256]{2,1,0:T(8,128)}) custom-call(f32[96,128]{1,0:T(8,128)} %bitcast.7, f32[32,128]{1,0:T(8,128)} %bitcast.8, s32[16]{0:T(128)} %bitcast.10), custom_call_target="tpu_custom_call" | custom-call | tf_op jit(solution)/shard_map/pallas_call | solution.py:161
  14.8 21.3 %shard_map.47 = (f32[16,256]{1,0:T(8,128)}, f32[240,256]{1,0:T(8,128)}) custom-call(s32[5,2,16]{2,1,0:T(2,128)} %bitcast.9, s32[16]{0:T(128)} %bitcast.11, f32[15,2,64,128]{3,2,1,0:T(8,128)} %get-tuple-element.9.far_ref), custom_call_target="tpu_custom_call" | custom-call | tf_op jit(solution)/shard_map/pallas_call | solution.py:485
  36.0 10.7 %shard_map.48 = f32[32,128]{1,0:T(8,128)} custom-call(f32[16,256]{1,0:T(8,128)} %get-tuple-element.10.gained_ref, f32[240,256]{1,0:T(8,128)} %get-tuple-element.11.handed_ref, f32[2,16,256]{2,1,0:T(8,128)} %get-tuple-element.12.over_ref), custom_call_target="tpu_custom_call" | custom-call | tf_op jit(solution)/shard_map/pallas_call | solution.py:573
  46.7 1.3 %broadcast_multiply_fusion = f32[32,128]{1,0:T(8,128)} fusion(f32[32,128]{1,0:T(8,128)} %shard_map.48), kind=kLoop, calls=%fused_computation | loop fusion | flops 4096 | bytes 32768 | tf_op jit(solution)/shard_map/mul | solution.py:599
